TPU v7x, 32 devices: a whole 2x2x4 slice. The times are simulated.
32 devices in a mesh: phi: 4 (over z), row: 2 (over core), theta: 4 (over y, x).
Axes of the slice: x: 2, y: 2, z: 4, core: 2. Of those that a mesh axis runs over, the one named last changes fastest.
Arguments:
- density: float32 [16, 32, 512], P('theta', 'row', 'phi'), may hold values from 0.5 to 2
- energy: float32 [16, 32, 512], P('theta', 'row', 'phi'), may hold values from 0.5 to 2.5
- velocity: float32 [3, 16, 32, 512], P(None, 'theta', 'row', 'phi'), may hold values from -1.2 to 1.2
- shifts: int32 [32], P('row'), may hold values from 0 to 511, as said below
- viscosity: float32 [32], P('row'), may hold values from 0.05 to 0.3
Outputs:
- density_out: float32 [16, 32, 512], P('theta', 'row', 'phi')
- energy_out: float32 [16, 32, 512], P('theta', 'row', 'phi')
- velocity_out: float32 [3, 16, 32, 512], P(None, 'theta', 'row', 'phi')
Inputs may be any that keep to these rules, and one draw needn't show every extreme that they name: `shifts`: in each aligned block of 16 radii at least one radius has an offset between 192 and 319, and at least one radius has an offset between 1 and 64.
All inputs are finite; a program needn't handle non-finite values.
Results may differ from a plain program's by a relative error of at most 0.00002.
Values sent between devices are 32-bit elements; how exact they have to be, the bound alone decides.
A program may use at most 64 MiB of HBM per device.

v0:
```python
import jax
import jax.numpy as jnp
from jax import lax
from jax.sharding import PartitionSpec as P

GAMMA_LESS = 0.4
TIME_STEP = 0.4
DAMPING = 1.0
ROTATION = 0.5


def padded_2(value, sides, width, wrap):
    for axis, dim in sides:
        devices, length = (lax.axis_size(axis), value.shape[dim])
        up = [(i, (i + 1) % devices) for i in range(devices if wrap else devices - 1)]
        down = [(j, i) for i, j in up]
        last = lax.slice_in_dim(value, length - width, length, axis=dim)
        first = lax.slice_in_dim(value, 0, width, axis=dim)
        before = lax.ppermute(last, axis, up)
        after = lax.ppermute(first, axis, down)
        value = jnp.concatenate([before, value, after], axis=dim)
    return value


def from_behind(value, axis, by):
    devices = lax.axis_size(axis)
    return lax.ppermute(value, axis, [(i, (i + by) % devices) for i in range(devices)])


def face_flux(quantity_lo, quantity_hi, speed_lo, speed_hi):
    return 0.25 * (speed_lo + speed_hi) * (quantity_lo + quantity_hi) - 0.5 * DAMPING * (
        quantity_hi - quantity_lo
    )


def segment_rates(padded, inv_rho):
    density, energy, radial_v, polar_v, azimuth_v = (
        padded[0],
        padded[1],
        padded[2],
        padded[3],
        padded[4],
    )

    def interior(quantity):
        return quantity[1:-1, 1:-1]

    def radial(quantity):
        fluxes = face_flux(
            quantity[1:-1, :-1], quantity[1:-1, 1:], radial_v[1:-1, :-1], radial_v[1:-1, 1:]
        )
        return fluxes[:, 1:] - fluxes[:, :-1]

    def polar(quantity):
        fluxes = face_flux(
            quantity[:-1, 1:-1], quantity[1:, 1:-1], polar_v[:-1, 1:-1], polar_v[1:, 1:-1]
        )
        return fluxes[1:] - fluxes[:-1]

    def laplace(quantity):
        return (
            quantity[2:, 1:-1]
            + quantity[:-2, 1:-1]
            + quantity[1:-1, 2:]
            + quantity[1:-1, :-2]
            - 4.0 * interior(quantity)
        )

    pressure = GAMMA_LESS * energy
    grad_radial = 0.5 * (pressure[1:-1, 2:] - pressure[1:-1, :-2])
    grad_polar = 0.5 * (pressure[2:, 1:-1] - pressure[:-2, 1:-1])
    rate_rho = -(radial(density) + polar(density))
    rate_energy = -(radial(energy) + polar(energy))
    rate_radial = (
        -grad_radial * inv_rho
        + 0.5 * DAMPING * laplace(radial_v)
        + 2.0 * ROTATION * interior(azimuth_v)
    )
    rate_polar = -grad_polar * inv_rho + 0.5 * DAMPING * laplace(polar_v)
    rate_azimuth = -(radial(azimuth_v) + polar(azimuth_v)) - 0.5 * ROTATION * interior(radial_v)
    return jnp.stack([rate_rho, rate_energy, rate_radial, rate_polar, rate_azimuth])


def with_rims(fields):
    return padded_2(fields, (("row", 2), ("theta", 1)), 1, False)


def per_device(density, energy, velocity, shifts, viscosity):
    fields = jnp.concatenate([density[None], energy[None], velocity], 0)
    inv_rho = 1.0 / density
    shard_len = density.shape[2]
    segment_one = fields + TIME_STEP * segment_rates(with_rims(fields), inv_rho)
    segment_two = 0.5 * (
        fields + segment_one + TIME_STEP * segment_rates(with_rims(segment_one), inv_rho)
    )
    shard_hops = shifts // shard_len
    remainder = shifts - shard_hops * shard_len
    rotated = segment_two
    for bit_index in range(lax.axis_size("phi").bit_length() - 1):
        hopped = from_behind(rotated, "phi", 1 << bit_index)
        chosen = shard_hops >> bit_index & 1 == 1
        rotated = jnp.where(chosen[None, None, :, None], hopped, rotated)
    further = from_behind(rotated, "phi", 1)
    combined = jnp.concatenate([further, rotated], 3)
    shifted = jax.vmap(
        lambda annulus, offset: lax.dynamic_slice_in_dim(
            annulus, shard_len - offset, shard_len, axis=2
        ),
        in_axes=(2, 0),
        out_axes=2,
    )(combined, remainder)
    padded = padded_2(shifted, (("phi", 3),), 1, True)
    behind = padded[..., :-2]
    ahead = padded[..., 2:]
    visc_coef = viscosity[None, :, None]
    velocity_out = shifted[2:] + visc_coef * (ahead[2:] - 2.0 * shifted[2:] + behind[2:])
    azimuth_slope = 0.5 * (ahead[4] - behind[4])
    energy_out = shifted[1] + visc_coef * shifted[0] * azimuth_slope * azimuth_slope
    return (shifted[0], energy_out, velocity_out)


def solution(mesh):
    return jax.shard_map(
        per_device,
        mesh=mesh,
        in_specs=(
            P("theta", "row", "phi"),
            P("theta", "row", "phi"),
            P(None, "theta", "row", "phi"),
            P("row"),
            P("row"),
        ),
        out_specs=(
            P("theta", "row", "phi"),
            P("theta", "row", "phi"),
            P(None, "theta", "row", "phi"),
        ),
        check_vma=False,
    )
```

profile of v0, /device:TPU:4, one launch (start us, length us, event | category | flops | bytes accessed | tf_op | source)
XLA Modules:
  0.0 87.4 jit_solution(4030833834008514777)
XLA Ops:
  0.7 1.0 %pad_maximum_fusion.1 = f32[5,4,16,128]{3,2,1,0:T(8,128)S(1)} fusion(f32[3,4,16,128]{3,2,1,0:T(8,128)} %param.7, f32[1,4,16,128]{3,2,1,0:T(8,128)} %bitcast.92, f32[1,4,16,128]{3,2,1,0:T(8,128)} %bitcast.89), kind=kLoop, calls=%fused_computation.4 | loop fusion | flops 81920 | bytes 327680 | tf_op jit(solution)/shard_map/concatenate | solution.py:89
  1.7 1.7 %collective-permute-start = (f32[5,4,1,128]{3,1,2,0:T(4,128)S(1)}, f32[5,4,1,128]{3,1,2,0:T(4,128)S(1)}, u32[]{:S(2)}, u32[]{:S(2)}) collective-permute-start(f32[5,4,1,128]{3,1,2,0:T(4,128)S(1)} %copy.1512), channel_id=1, source_target_pairs={{0,4},{1,5},{2,6},{3,7},{8,12},{9,13},{10,14},{11,15},{16,20},{17,... | collective-permute-start | bytes 30728 | tf_op jit(solution)/shard_map/ppermute | solution.py:19
  3.4 1.3 %collective-permute-start.1 = (f32[5,4,1,128]{3,1,2,0:T(4,128)S(1)}, f32[5,4,1,128]{3,1,2,0:T(4,128)S(1)}, u32[]{:S(2)}, u32[]{:S(2)}) collective-permute-start(f32[5,4,1,128]{3,1,2,0:T(4,128)S(1)} %copy.1513), channel_id=1, source_target_pairs={{4,0},{5,1},{6,2},{7,3},{12,8},{13,9},{14,10},{15,11},{20,16},{21,... | collective-permute-start | bytes 30728 | tf_op jit(solution)/shard_map/ppermute | solution.py:20
  4.8 1.7 %collective-permute-done.1 = f32[5,4,1,128]{3,1,2,0:T(4,128)S(1)} collective-permute-done((f32[5,4,1,128]{3,1,2,0:T(4,128)S(1)}, f32[5,4,1,128]{3,1,2,0:T(4,128)S(1)}, u32[]{:S(2)}, u32[]{:S(2)}) %collective-permute-start.1) | collective-permute-done | bytes 10272 | tf_op jit(solution)/shard_map/ppermute | solution.py:20
  6.6 3.4 %collective-permute-start.2 = (f32[5,1,18,128]{3,1,2,0:T(1,128)S(1)}, f32[5,1,18,128]{3,1,2,0:T(1,128)S(1)}, u32[]{:S(2)}, u32[]{:S(2)}) collective-permute-start(f32[5,1,18,128]{3,1,2,0:T(1,128)S(1)} %get-tuple-element.92), channel_id=1, source_target_pairs={{0,1},{1,2},{2,3},{4,5},{5,6},{6,7},{8,9},{9,10},{10,11},{12,13},{... | collective-permute-start | bytes 138248 | tf_op jit(solution)/shard_map/ppermute | solution.py:19
  10.0 3.3 %collective-permute-start.3 = (f32[5,1,18,128]{3,1,2,0:T(1,128)S(1)}, f32[5,1,18,128]{3,1,2,0:T(1,128)S(1)}, u32[]{:S(2)}, u32[]{:S(2)}) collective-permute-start(f32[5,1,18,128]{3,1,2,0:T(1,128)S(1)} %get-tuple-element.91), channel_id=1, source_target_pairs={{1,0},{2,1},{3,2},{5,4},{6,5},{7,6},{9,8},{10,9},{11,10},{13,12},{... | collective-permute-start | bytes 138248 | tf_op jit(solution)/shard_map/ppermute | solution.py:20
  13.5 2.5 %collective-permute-done.3 = f32[5,1,18,128]{3,1,2,0:T(1,128)S(1)} collective-permute-done((f32[5,1,18,128]{3,1,2,0:T(1,128)S(1)}, f32[5,1,18,128]{3,1,2,0:T(1,128)S(1)}, u32[]{:S(2)}, u32[]{:S(2)}) %collective-permute-start.3) | collective-permute-done | bytes 46112 | tf_op jit(solution)/shard_map/ppermute | solution.py:20
  18.7 1.3 %collective-permute-start.4 = (f32[5,4,1,128]{3,2,1,0:T(1,128)S(1)}, f32[5,4,1,128]{3,2,1,0:T(1,128)S(1)}, u32[]{:S(2)}, u32[]{:S(2)}) collective-permute-start(f32[5,4,1,128]{3,2,1,0:T(1,128)S(1)} %get-tuple-element.95), channel_id=1, source_target_pairs={{0,4},{1,5},{2,6},{3,7},{8,12},{9,13},{10,14},{11,15},{16,20},{17,... | collective-permute-start | bytes 30728 | tf_op jit(solution)/shard_map/ppermute | solution.py:19
  20.0 1.3 %collective-permute-start.5 = (f32[5,4,1,128]{3,2,1,0:T(1,128)S(1)}, f32[5,4,1,128]{3,2,1,0:T(1,128)S(1)}, u32[]{:S(2)}, u32[]{:S(2)}) collective-permute-start(f32[5,4,1,128]{3,2,1,0:T(1,128)S(1)} %get-tuple-element.96), channel_id=1, source_target_pairs={{4,0},{5,1},{6,2},{7,3},{12,8},{13,9},{14,10},{15,11},{20,16},{21,... | collective-permute-start | bytes 30728 | tf_op jit(solution)/shard_map/ppermute | solution.py:20
  21.3 1.8 %collective-permute-done.5 = f32[5,4,1,128]{3,2,1,0:T(1,128)S(1)} collective-permute-done((f32[5,4,1,128]{3,2,1,0:T(1,128)S(1)}, f32[5,4,1,128]{3,2,1,0:T(1,128)S(1)}, u32[]{:S(2)}, u32[]{:S(2)}) %collective-permute-start.5) | collective-permute-done | bytes 10272 | tf_op jit(solution)/shard_map/ppermute | solution.py:20
  23.2 4.2 %collective-permute-start.7 = (f32[5,1,18,128]{3,1,2,0:T(1,128)S(1)}, f32[5,1,18,128]{3,1,2,0:T(1,128)S(1)}, u32[]{:S(2)}, u32[]{:S(2)}) collective-permute-start(f32[5,1,18,128]{3,1,2,0:T(1,128)S(1)} %copy.1503), channel_id=1, source_target_pairs={{1,0},{2,1},{3,2},{5,4},{6,5},{7,6},{9,8},{10,9},{11,10},{13,12},{... | collective-permute-start | bytes 138248 | tf_op jit(solution)/shard_map/ppermute | solution.py:20
  27.5 1.9 %collective-permute-start.6 = (f32[5,1,18,128]{3,1,2,0:T(1,128)S(1)}, f32[5,1,18,128]{3,1,2,0:T(1,128)S(1)}, u32[]{:S(2)}, u32[]{:S(2)}) collective-permute-start(f32[5,1,18,128]{3,1,2,0:T(1,128)S(1)} %copy.1502), channel_id=1, source_target_pairs={{0,1},{1,2},{2,3},{4,5},{5,6},{6,7},{8,9},{9,10},{10,11},{12,13},{... | collective-permute-start | bytes 138248 | tf_op jit(solution)/shard_map/ppermute | solution.py:19
  30.1 4.2 %collective-permute-done.6 = f32[5,1,18,128]{3,1,2,0:T(1,128)S(1)} collective-permute-done((f32[5,1,18,128]{3,1,2,0:T(1,128)S(1)}, f32[5,1,18,128]{3,1,2,0:T(1,128)S(1)}, u32[]{:S(2)}, u32[]{:S(2)}) %collective-permute-start.6) | collective-permute-done | bytes 46112 | tf_op jit(solution)/shard_map/ppermute | solution.py:19
  34.8 1.6 %collective-permute-start.8 = (f32[5,4,16,128]{3,2,1,0:T(8,128)S(1)}, f32[5,4,16,128]{3,2,1,0:T(8,128)S(1)}, u32[]{:S(2)}, u32[]{:S(2)}) collective-permute-start(f32[5,4,16,128]{3,2,1,0:T(8,128)S(1)} %add_multiply_fusion), channel_id=1, source_target_pairs={{0,8},{8,16},{16,24},{24,0},{1,9},{9,17},{17,25},{25,1},{2,10},{10... | collective-permute-start | bytes 491528 | tf_op jit(solution)/shard_map/ppermute | solution.py:27
  36.4 5.5 %collective-permute-done.8 = f32[5,4,16,128]{3,2,1,0:T(8,128)S(1)} collective-permute-done((f32[5,4,16,128]{3,2,1,0:T(8,128)S(1)}, f32[5,4,16,128]{3,2,1,0:T(8,128)S(1)}, u32[]{:S(2)}, u32[]{:S(2)}) %collective-permute-start.8) | collective-permute-done | bytes 163872 | tf_op jit(solution)/shard_map/ppermute | solution.py:27
  42.9 6.5 %collective-permute-done.9 = f32[5,4,16,128]{3,2,1,0:T(8,128)S(1)} collective-permute-done((f32[5,4,16,128]{3,2,1,0:T(8,128)S(1)}, f32[5,4,16,128]{3,2,1,0:T(8,128)S(1)}, u32[]{:S(2)}, u32[]{:S(2)}) %collective-permute-start.9) | collective-permute-done | bytes 163872 | tf_op jit(solution)/shard_map/ppermute | solution.py:27
  49.5 1.4 %collective-permute-start.10 = (f32[5,4,16,128]{3,2,1,0:T(8,128)S(1)}, f32[5,4,16,128]{3,2,1,0:T(8,128)S(1)}, u32[]{:S(2)}, u32[]{:S(2)}) collective-permute-start(f32[5,4,16,128]{3,2,1,0:T(8,128)S(1)} %broadcast_select_fusion.1), channel_id=1, source_target_pairs={{0,8},{8,16},{16,24},{24,0},{1,9},{9,17},{17,25},{25,1},{2,10},{10... | collective-permute-start | bytes 491528 | tf_op jit(solution)/shard_map/ppermute | solution.py:27
  50.9 6.1 %collective-permute-done.10 = f32[5,4,16,128]{3,2,1,0:T(8,128)S(1)} collective-permute-done((f32[5,4,16,128]{3,2,1,0:T(8,128)S(1)}, f32[5,4,16,128]{3,2,1,0:T(8,128)S(1)}, u32[]{:S(2)}, u32[]{:S(2)}) %collective-permute-start.10) | collective-permute-done | bytes 163872 | tf_op jit(solution)/shard_map/ppermute | solution.py:27
  57.1 7.7 %copy.1506 = f32[16,5,4,256]{1,2,0,3:T(4,128)} copy(f32[16,5,4,256]{3,0,2,1:T(8,128)S(1)} %maximum_bitcast_fusion) | data formatting | bytes 655360 | tf_op jit(solution)/shard_map/vmap()/transpose | solution.py:106
  64.8 9.0 %gather_fusion = f32[16,5,4,128]{1,2,3,0:T(4,128)} fusion(f32[16,5,4,256]{1,2,0,3:T(4,128)} %copy.1506, s32[16]{0:T(128)S(1)} %get-tuple-element.77), kind=kCustom, calls=%fused_computation | custom fusion | bytes 327936 | tf_op jit(solution)/shard_map/vmap()/gather | solution.py:106
  73.8 2.9 %copy.1507 = f32[16,5,4,128]{3,0,2,1:T(8,128)S(1)} copy(f32[16,5,4,128]{1,2,3,0:T(4,128)} %gather_fusion) | data formatting | bytes 327680 | tf_op jit(solution)/shard_map/vmap()/gather | solution.py:106
  76.7 2.1 %collective-permute-start.11 = (f32[5,4,16,1]{3,2,1,0:T(8,128)S(1)}, f32[5,4,16,1]{3,2,1,0:T(8,128)S(1)}, u32[]{:S(2)}, u32[]{:S(2)}) collective-permute-start(f32[5,4,16,1]{3,2,1,0:T(8,128)S(1)} %get-tuple-element.93), channel_id=1, source_target_pairs={{8,0},{16,8},{24,16},{0,24},{9,1},{17,9},{25,17},{1,25},{10,2},{18... | collective-permute-start | bytes 3848 | tf_op jit(solution)/shard_map/ppermute | solution.py:20
  78.8 3.5 %collective-permute-done.11 = f32[5,4,16,1]{3,2,1,0:T(8,128)S(1)} collective-permute-done((f32[5,4,16,1]{3,2,1,0:T(8,128)S(1)}, f32[5,4,16,1]{3,2,1,0:T(8,128)S(1)}, u32[]{:S(2)}, u32[]{:S(2)}) %collective-permute-start.11) | collective-permute-done | bytes 1312 | tf_op jit(solution)/shard_map/ppermute | solution.py:20
  82.3 3.6 %collective-permute-done.12 = f32[5,4,16,1]{3,2,1,0:T(8,128)S(1)} collective-permute-done((f32[5,4,16,1]{3,2,1,0:T(8,128)S(1)}, f32[5,4,16,1]{3,2,1,0:T(8,128)S(1)}, u32[]{:S(2)}, u32[]{:S(2)}) %collective-permute-start.12) | collective-permute-done | bytes 1312 | tf_op jit(solution)/shard_map/ppermute | solution.py:19
  (59 shorter events, 6.9 us)
Async XLA Ops:
  0.6 34.0 %copy-start = (f32[4,16,128]{2,1,0:T(8,128)S(1)}, f32[4,16,128]{2,1,0:T(8,128)}, u32[]{:S(2)}) copy-start(f32[4,16,128]{2,1,0:T(8,128)} %param.5) | copy-start | bytes 98308
  0.6 34.1 %copy-start.1 = (f32[3,4,16,128]{3,2,1,0:T(8,128)S(1)}, f32[3,4,16,128]{3,2,1,0:T(8,128)}, u32[]{:S(2)}) copy-start(f32[3,4,16,128]{3,2,1,0:T(8,128)} %param.7) | copy-start | bytes 294916
  0.7 34.1 %copy-start.2 = (f32[4,16,128]{2,1,0:T(8,128)S(1)}, f32[4,16,128]{2,1,0:T(8,128)}, u32[]{:S(2)}) copy-start(f32[4,16,128]{2,1,0:T(8,128)} %param.6) | copy-start | bytes 98308
  1.7 3.1 %collective-permute-start = (f32[5,4,1,128]{3,1,2,0:T(4,128)S(1)}, f32[5,4,1,128]{3,1,2,0:T(4,128)S(1)}, u32[]{:S(2)}, u32[]{:S(2)}) collective-permute-start(f32[5,4,1,128]{3,1,2,0:T(4,128)S(1)} %copy.1512), channel_id=1, source_target_pairs={{0,4},{1,5},{2,6},{3,7},{8,12},{9,13},{10,14},{11,15},{16,20},{17,... | collective-permute-start | bytes 30728 | tf_op jit(solution)/shard_map/ppermute | solution.py:19
  3.4 3.1 %collective-permute-start.1 = (f32[5,4,1,128]{3,1,2,0:T(4,128)S(1)}, f32[5,4,1,128]{3,1,2,0:T(4,128)S(1)}, u32[]{:S(2)}, u32[]{:S(2)}) collective-permute-start(f32[5,4,1,128]{3,1,2,0:T(4,128)S(1)} %copy.1513), channel_id=1, source_target_pairs={{4,0},{5,1},{6,2},{7,3},{12,8},{13,9},{14,10},{15,11},{20,16},{21,... | collective-permute-start | bytes 30728 | tf_op jit(solution)/shard_map/ppermute | solution.py:20
  6.6 6.8 %collective-permute-start.2 = (f32[5,1,18,128]{3,1,2,0:T(1,128)S(1)}, f32[5,1,18,128]{3,1,2,0:T(1,128)S(1)}, u32[]{:S(2)}, u32[]{:S(2)}) collective-permute-start(f32[5,1,18,128]{3,1,2,0:T(1,128)S(1)} %get-tuple-element.92), channel_id=1, source_target_pairs={{0,1},{1,2},{2,3},{4,5},{5,6},{6,7},{8,9},{9,10},{10,11},{12,13},{... | collective-permute-start | bytes 138248 | tf_op jit(solution)/shard_map/ppermute | solution.py:19
  10.0 6.0 %collective-permute-start.3 = (f32[5,1,18,128]{3,1,2,0:T(1,128)S(1)}, f32[5,1,18,128]{3,1,2,0:T(1,128)S(1)}, u32[]{:S(2)}, u32[]{:S(2)}) collective-permute-start(f32[5,1,18,128]{3,1,2,0:T(1,128)S(1)} %get-tuple-element.91), channel_id=1, source_target_pairs={{1,0},{2,1},{3,2},{5,4},{6,5},{7,6},{9,8},{10,9},{11,10},{13,12},{... | collective-permute-start | bytes 138248 | tf_op jit(solution)/shard_map/ppermute | solution.py:20
  18.7 2.6 %collective-permute-start.4 = (f32[5,4,1,128]{3,2,1,0:T(1,128)S(1)}, f32[5,4,1,128]{3,2,1,0:T(1,128)S(1)}, u32[]{:S(2)}, u32[]{:S(2)}) collective-permute-start(f32[5,4,1,128]{3,2,1,0:T(1,128)S(1)} %get-tuple-element.95), channel_id=1, source_target_pairs={{0,4},{1,5},{2,6},{3,7},{8,12},{9,13},{10,14},{11,15},{16,20},{17,... | collective-permute-start | bytes 30728 | tf_op jit(solution)/shard_map/ppermute | solution.py:19
  20.0 3.1 %collective-permute-start.5 = (f32[5,4,1,128]{3,2,1,0:T(1,128)S(1)}, f32[5,4,1,128]{3,2,1,0:T(1,128)S(1)}, u32[]{:S(2)}, u32[]{:S(2)}) collective-permute-start(f32[5,4,1,128]{3,2,1,0:T(1,128)S(1)} %get-tuple-element.96), channel_id=1, source_target_pairs={{4,0},{5,1},{6,2},{7,3},{12,8},{13,9},{14,10},{15,11},{20,16},{21,... | collective-permute-start | bytes 30728 | tf_op jit(solution)/shard_map/ppermute | solution.py:20
  23.2 6.9 %collective-permute-start.7 = (f32[5,1,18,128]{3,1,2,0:T(1,128)S(1)}, f32[5,1,18,128]{3,1,2,0:T(1,128)S(1)}, u32[]{:S(2)}, u32[]{:S(2)}) collective-permute-start(f32[5,1,18,128]{3,1,2,0:T(1,128)S(1)} %copy.1503), channel_id=1, source_target_pairs={{1,0},{2,1},{3,2},{5,4},{6,5},{7,6},{9,8},{10,9},{11,10},{13,12},{... | collective-permute-start | bytes 138248 | tf_op jit(solution)/shard_map/ppermute | solution.py:20
  27.5 6.8 %collective-permute-start.6 = (f32[5,1,18,128]{3,1,2,0:T(1,128)S(1)}, f32[5,1,18,128]{3,1,2,0:T(1,128)S(1)}, u32[]{:S(2)}, u32[]{:S(2)}) collective-permute-start(f32[5,1,18,128]{3,1,2,0:T(1,128)S(1)} %copy.1502), channel_id=1, source_target_pairs={{0,1},{1,2},{2,3},{4,5},{5,6},{6,7},{8,9},{9,10},{10,11},{12,13},{... | collective-permute-start | bytes 138248 | tf_op jit(solution)/shard_map/ppermute | solution.py:19
  34.6 51.3 %copy-start.3 = (f32[16]{0:T(128)S(1)}, f32[16]{0:T(128)}, u32[]{:S(2)}) copy-start(f32[16]{0:T(128)} %param.9) | copy-start | bytes 196
  34.8 7.2 %collective-permute-start.8 = (f32[5,4,16,128]{3,2,1,0:T(8,128)S(1)}, f32[5,4,16,128]{3,2,1,0:T(8,128)S(1)}, u32[]{:S(2)}, u32[]{:S(2)}) collective-permute-start(f32[5,4,16,128]{3,2,1,0:T(8,128)S(1)} %add_multiply_fusion), channel_id=1, source_target_pairs={{0,8},{8,16},{16,24},{24,0},{1,9},{9,17},{17,25},{25,1},{2,10},{10... | collective-permute-start | bytes 491528 | tf_op jit(solution)/shard_map/ppermute | solution.py:27
  42.0 7.4 %collective-permute-start.9 = (f32[5,4,16,128]{3,2,1,0:T(8,128)S(1)}, f32[5,4,16,128]{3,2,1,0:T(8,128)S(1)}, u32[]{:S(2)}, u32[]{:S(2)}) collective-permute-start(f32[5,4,16,128]{3,2,1,0:T(8,128)S(1)} %broadcast_select_fusion), channel_id=1, source_target_pairs={{0,16},{8,24},{16,0},{24,8},{1,17},{9,25},{17,1},{25,9},{2,18},{10... | collective-permute-start | bytes 491528 | tf_op jit(solution)/shard_map/ppermute | solution.py:27
  49.5 7.5 %collective-permute-start.10 = (f32[5,4,16,128]{3,2,1,0:T(8,128)S(1)}, f32[5,4,16,128]{3,2,1,0:T(8,128)S(1)}, u32[]{:S(2)}, u32[]{:S(2)}) collective-permute-start(f32[5,4,16,128]{3,2,1,0:T(8,128)S(1)} %broadcast_select_fusion.1), channel_id=1, source_target_pairs={{0,8},{8,16},{16,24},{24,0},{1,9},{9,17},{17,25},{25,1},{2,10},{10... | collective-permute-start | bytes 491528 | tf_op jit(solution)/shard_map/ppermute | solution.py:27
  76.7 5.6 %collective-permute-start.11 = (f32[5,4,16,1]{3,2,1,0:T(8,128)S(1)}, f32[5,4,16,1]{3,2,1,0:T(8,128)S(1)}, u32[]{:S(2)}, u32[]{:S(2)}) collective-permute-start(f32[5,4,16,1]{3,2,1,0:T(8,128)S(1)} %get-tuple-element.93), channel_id=1, source_target_pairs={{8,0},{16,8},{24,16},{0,24},{9,1},{17,9},{25,17},{1,25},{10,2},{18... | collective-permute-start | bytes 3848 | tf_op jit(solution)/shard_map/ppermute | solution.py:20
  78.8 7.1 %collective-permute-start.12 = (f32[5,4,16,1]{3,2,1,0:T(8,128)S(1)}, f32[5,4,16,1]{3,2,1,0:T(8,128)S(1)}, u32[]{:S(2)}, u32[]{:S(2)}) collective-permute-start(f32[5,4,16,1]{3,2,1,0:T(8,128)S(1)} %get-tuple-element.94), channel_id=1, source_target_pairs={{0,8},{8,16},{16,24},{24,0},{1,9},{9,17},{17,25},{25,1},{2,10},{10... | collective-permute-start | bytes 3848 | tf_op jit(solution)/shard_map/ppermute | solution.py:19
where the time goes:
time: 88 us; the launch traced here: 87.4 us
  waiting for transfers between devices  35.5 us (40%)
  starting transfers between devices  24.5 us (28%)
  local copies, waits for them, and re-layouts  20.1 us (23%)
  other arithmetic  6.36 us (7%)
  between operations  1 us (1%)
    ppermute x3, waiting for transfers between devices, from_behind(): lax.ppermute(value, axis, [(i, (i + by) % devices) for i in range(devices)])  18.2 us
    ppermute x5, starting transfers between devices, padded_2(): after = lax.ppermute(first, axis, down)  12.2 us
    gather x2, local copies, waits for them, and re-layouts, per_device(): lax.dynamic_slice_in_dim(annulus, shard_len - offset, shard_len, axis=2)  11.9 us
    ppermute x5, waiting for transfers between devices, padded_2(): after = lax.ppermute(first, axis, down)  9.44 us
    ppermute x5, starting transfers between devices, padded_2(): before = lax.ppermute(last, axis, up)  8.36 us
    ppermute x5, waiting for transfers between devices, padded_2(): before = lax.ppermute(last, axis, up)  7.9 us
    transpose x1, local copies, waits for them, and re-layouts, per_device(): lax.dynamic_slice_in_dim(annulus, shard_len - offset, shard_len, axis=2)  7.68 us
    ppermute x3, starting transfers between devices, from_behind(): lax.ppermute(value, axis, [(i, (i + by) % devices) for i in range(devices)])  3.92 us
  transfers between devices with their start and end apart: 13, of which 10 were waited for; matrix products, arithmetic and copies ran while one was open for 1% of the time, Pallas kernels for 0%

commit v1 on v0

v1 whole, which is shorter than its diff:
```python
import functools

import jax
import jax.numpy as jnp
from jax import lax
from jax.experimental import pallas as pl
from jax.experimental.pallas import tpu as pltpu
from jax.sharding import PartitionSpec as P

GAMMA_LESS = 0.4
TIME_STEP = 0.4
DAMPING = 1.0
ROTATION = 0.5
TILE = 8
FIELDS = 5
MESH = pl.DeviceIdType.MESH


def face_flux(quantity_lo, quantity_hi, speed_lo, speed_hi):
    return 0.25 * (speed_lo + speed_hi) * (quantity_lo + quantity_hi) - 0.5 * DAMPING * (
        quantity_hi - quantity_lo
    )


def rates(src, t, first, count, inv_rho):
    def layer(step_t, step_r):
        return [src[f, t + step_t, pl.ds(first + step_r, count)] for f in range(FIELDS)]

    mid, inner, outer = layer(0, 0), layer(0, -1), layer(0, 1)
    low, high = layer(-1, 0), layer(1, 0)

    def div(q):
        return (
            face_flux(mid[q], outer[q], mid[2], outer[2])
            - face_flux(inner[q], mid[q], inner[2], mid[2])
        ) + (face_flux(mid[q], high[q], mid[3], high[3]) - face_flux(low[q], mid[q], low[3], mid[3]))

    def laplace(q):
        return high[q] + low[q] + outer[q] + inner[q] - 4.0 * mid[q]

    grad_radial = 0.5 * (GAMMA_LESS * outer[1] - GAMMA_LESS * inner[1])
    grad_polar = 0.5 * (GAMMA_LESS * high[1] - GAMMA_LESS * low[1])
    out = [
        -div(0),
        -div(1),
        -grad_radial * inv_rho + 0.5 * DAMPING * laplace(2) + 2.0 * ROTATION * mid[4],
        -grad_polar * inv_rho + 0.5 * DAMPING * laplace(3),
        -div(4) - 0.5 * ROTATION * mid[2],
    ]
    return mid, out


def kernel(
    sizes,
    shifts,
    viscosity,
    density,
    energy,
    velocity,
    density_out,
    energy_out,
    velocity_out,
    state,
    mid_state,
    ring,
    halo_send,
    halo_recv,
    ring_send,
    ring_recv,
):
    n_phi, n_row, n_theta = sizes
    slabs, rows, lanes = density.shape
    phi, row, theta = (lax.axis_index(a) for a in ("phi", "row", "theta"))
    own_t, own_r = pl.ds(2, slabs), pl.ds(TILE, rows)
    ahead_phi = lax.rem(phi + 1, n_phi)
    back_phi = lax.rem(phi + n_phi - 1, n_phi)

    steps = [(0, 1), (0, -1), (1, 1), (1, -1), (-1, 1), (-1, -1), (1, 0), (-1, 0)]
    if n_row == 1:
        steps = [s for s in steps if s[0] == 0]
    if n_theta == 1:
        steps = [s for s in steps if s[1] == 0]

    def exists(step):
        r, t = row + step[0], theta + step[1]
        return (r >= 0) & (r < n_row) & (t >= 0) & (t < n_theta)

    barrier = pltpu.get_barrier_semaphore()
    for step in steps:

        @pl.when(exists(step))
        def _():
            pl.semaphore_signal(
                barrier,
                inc=1,
                device_id={"row": row + step[0], "theta": theta + step[1]},
                device_id_type=MESH,
            )

    if n_phi > 1:
        for other in (ahead_phi, back_phi):
            pl.semaphore_signal(barrier, inc=1, device_id={"phi": other}, device_id_type=MESH)

    state[0, own_t, own_r] = density[...]
    state[1, own_t, own_r] = energy[...]
    for f in range(3):
        state[2 + f, own_t, own_r] = velocity[f]

    def region(step):
        r, t = step
        src_r = {0: pl.ds(0, rows), 1: pl.ds(rows - TILE, TILE), -1: pl.ds(0, TILE)}[r]
        dst_r = {0: own_r, 1: pl.ds(0, TILE), -1: pl.ds(TILE + rows, TILE)}[r]
        deep = 2 if r == 0 else 1
        src_t = {0: pl.ds(0, slabs), 1: pl.ds(slabs - deep, deep), -1: pl.ds(0, deep)}[t]
        dst_t = {0: own_t, 1: pl.ds(2 - deep, deep), -1: pl.ds(2 + slabs, deep)}[t]
        return src_t, src_r, dst_t, dst_r

    def copies(step):
        k = steps.index(step)
        src_t, src_r, dst_t, dst_r = region(step)
        pairs = [
            (density.at[src_t, src_r], state.at[0, dst_t, dst_r]),
            (energy.at[src_t, src_r], state.at[1, dst_t, dst_r]),
            (velocity.at[:, src_t, src_r], state.at[pl.ds(2, 3), dst_t, dst_r]),
        ]
        return [
            pltpu.make_async_remote_copy(
                src_ref=src,
                dst_ref=dst,
                send_sem=halo_send.at[k, i],
                recv_sem=halo_recv.at[k, i],
                device_id={"row": row + step[0], "theta": theta + step[1]},
                device_id_type=MESH,
            )
            for i, (src, dst) in enumerate(pairs)
        ]

    zero_from = [(0, 1), (0, -1), (1, 1), (1, -1), (-1, 1), (-1, -1), (1, 0), (-1, 0)]
    for step in zero_from:
        _, _, dst_t, dst_r = region(step)
        opposite = (-step[0], -step[1])

        def clear():
            for f in range(FIELDS):
                state[f, dst_t, dst_r] = jnp.zeros((dst_t.size, dst_r.size, lanes), jnp.float32)

        if opposite in steps:
            pl.when(jnp.logical_not(exists(opposite)))(clear)
        else:
            clear()

    expected = 2 if n_phi > 1 else 0
    for step in steps:
        expected = expected + exists(step).astype(jnp.int32)
    pl.semaphore_wait(barrier, expected)

    for step in steps:

        @pl.when(exists(step))
        def _():
            for copy in copies(step):
                copy.start()

    for step in steps:

        @pl.when(exists((-step[0], -step[1])))
        def _():
            for copy in copies(step):
                copy.wait_recv()

    for t in range(1, slabs + 3):
        inside = 2 <= t < slabs + 2
        first, count = (TILE - 1, rows + 2) if inside else (TILE, rows)
        inv_rho = 1.0 / state[0, t, pl.ds(first, count)]
        mid, rate = rates(state, t, first, count, inv_rho)
        for f in range(FIELDS):
            mid_state[f, t, pl.ds(first, count)] = mid[f] + TIME_STEP * rate[f]

    for at, edge in ((1, theta == 0), (slabs + 2, theta == n_theta - 1)):

        @pl.when(edge)
        def _():
            for f in range(FIELDS):
                mid_state[f, at, own_r] = jnp.zeros((rows, lanes), jnp.float32)

    for at, edge in ((TILE - 1, row == 0), (TILE + rows, row == n_row - 1)):

        @pl.when(edge)
        def _():
            for f in range(FIELDS):
                mid_state[f, own_t, pl.ds(at, 1)] = jnp.zeros((slabs, 1, lanes), jnp.float32)

    for t in range(slabs):
        inv_rho = 1.0 / state[0, t + 2, own_r]
        mid, rate = rates(mid_state, t + 2, TILE, rows, inv_rho)
        for f in range(FIELDS):
            ring[phi, t, f] = 0.5 * (state[f, t + 2, own_r] + mid[f] + TIME_STEP * rate[f])

    half = slabs // 2
    parts = [pl.ds(0, half), pl.ds(half, slabs - half)]

    def hop(way, distance, part):
        sign = 1 if way == 0 else -1
        slot = lax.rem(phi + n_phi - sign * (distance - 1), n_phi)
        return pltpu.make_async_remote_copy(
            src_ref=ring.at[slot, parts[part]],
            dst_ref=ring.at[slot, parts[part]],
            send_sem=ring_send.at[way, distance - 1, part],
            recv_sem=ring_recv.at[way, distance - 1, part],
            device_id={"phi": ahead_phi if way == 0 else back_phi},
            device_id_type=MESH,
        )

    last = n_phi // 2
    sends = []
    for distance in range(1, last + 1):
        for order in (0, 1):
            for way in (0, 1):
                part = order ^ way
                if distance > 1:
                    hop(way, distance - 1, part).wait_recv()
                if distance == last and n_phi % 2 == 0 and order == 1:
                    continue
                sends.append(hop(way, distance, part))
                sends[-1].start()
    if n_phi > 1:
        for order in (0, 1):
            for way in (0, 1):
                if n_phi % 2 == 0 and order == 1:
                    continue
                hop(way, last, order ^ way).wait_recv()

    lane = lax.broadcasted_iota(jnp.int32, (rows, lanes), 1)
    line = lax.broadcasted_iota(jnp.int32, (rows, lanes), 0)
    hops = jnp.zeros((rows, lanes), jnp.int32)
    rest = jnp.zeros((rows, lanes), jnp.int32)
    visc = jnp.zeros((rows, lanes), jnp.float32)
    for r in range(rows):
        shift = shifts[r]
        count = lax.div(shift, lanes)
        hops = jnp.where(line == r, count, hops)
        rest = jnp.where(line == r, shift - count * lanes, rest)
        visc = jnp.where(line == r, viscosity[r], visc)
    near = phi - hops
    near = jnp.where(near < 0, near + n_phi, near)
    far = jnp.where(near == 0, n_phi - 1, near - 1)
    next_ = jnp.where(near == n_phi - 1, 0, near + 1)
    from_near = lane < lanes - rest
    whole_first = (rest == 0) & (lane == 0)
    main_slot = jnp.where(from_near, near, far)
    side_slot = jnp.where(from_near, jnp.where(whole_first, next_, far), near)
    index = jnp.where(lane >= rest, lane - rest, lane - rest + lanes)

    def turned(slot_of, t, f):
        value = ring[0, t, f]
        for slot in range(1, n_phi):
            value = jnp.where(slot_of == slot, ring[slot, t, f], value)
        return jnp.take_along_axis(value, index, axis=1, mode="promise_in_bounds")

    for t in range(slabs):
        dens = turned(main_slot, t, 0)
        ener = turned(main_slot, t, 1)
        density_out[t] = dens
        for f in range(3):
            here = turned(main_slot, t, 2 + f)
            side = turned(side_slot, t, 2 + f)
            behind = pltpu.roll(jnp.where(lane == lanes - 1, side, here), 1, 1)
            ahead = pltpu.roll(jnp.where(lane == 0, side, here), lanes - 1, 1)
            velocity_out[f, t] = here + visc * (ahead - 2.0 * here + behind)
            if f == 2:
                slope = 0.5 * (ahead - behind)
                energy_out[t] = ener + visc * dens * slope * slope

    for step in steps:

        @pl.when(exists(step))
        def _():
            for copy in copies(step):
                copy.wait_send()

    for send in sends:
        send.wait_send()


def per_device(sizes, density, energy, velocity, shifts, viscosity):
    slabs, rows, lanes = density.shape
    n_phi = sizes[0]
    padded = (FIELDS, slabs + 4, rows + 2 * TILE, lanes)
    in_vmem = pl.BlockSpec(memory_space=pltpu.VMEM)
    in_smem = pl.BlockSpec(memory_space=pltpu.SMEM)
    reach = max(n_phi // 2, 1)
    return pl.pallas_call(
        functools.partial(kernel, sizes),
        out_shape=[jax.ShapeDtypeStruct(v.shape, v.dtype) for v in (density, energy, velocity)],
        in_specs=[in_smem, in_smem, in_vmem, in_vmem, in_vmem],
        out_specs=[in_vmem] * 3,
        scratch_shapes=[
            pltpu.VMEM(padded, jnp.float32),
            pltpu.VMEM(padded, jnp.float32),
            pltpu.VMEM((n_phi, slabs, FIELDS, rows, lanes), jnp.float32),
            pltpu.SemaphoreType.DMA((8, 3)),
            pltpu.SemaphoreType.DMA((8, 3)),
            pltpu.SemaphoreType.DMA((2, reach, 2)),
            pltpu.SemaphoreType.DMA((2, reach, 2)),
        ],
        compiler_params=pltpu.CompilerParams(collective_id=0, has_side_effects=True),
        name="disc_step",
    )(shifts, viscosity, density, energy, velocity)


def solution(mesh):
    sizes = tuple(mesh.shape[a] for a in ("phi", "row", "theta"))
    cells = P("theta", "row", "phi")
    vectors = P(None, "theta", "row", "phi")
    return jax.shard_map(
        functools.partial(per_device, sizes),
        mesh=mesh,
        in_specs=(cells, cells, vectors, P("row"), P("row")),
        out_specs=(cells, cells, vectors),
        check_vma=False,
    )
```

time: 88 us -> 30.7 us (0.35)
  the two profiles are of different devices: /device:TPU:4 before, /device:TPU:0 now
where the time goes in v1:
time: 30.7 us; the launch traced here: 30.4 us
  Pallas kernels  26.4 us (86%)
  local copies, waits for them, and re-layouts  3.43 us (11%)
  between operations  0.65 us (2%)
    pallas_call x1, Pallas kernels, per_device(): pl.pallas_call(functools.partial(kernel, sizes), out_shape=[jax.ShapeDtyp...  26.4 us
    unnamed x5, local copies, waits for them, and re-layouts  3.43 us

profile of v1, /device:TPU:0, one launch (start us, length us, event | category | flops | bytes accessed | tf_op | source)
XLA Modules:
  0.0 30.4 jit_solution(16512907271317377176)
XLA Ops:
  0.6 26.4 %disc_step.1 = (f32[4,16,128]{2,1,0:T(8,128)}, f32[4,16,128]{2,1,0:T(8,128)}, f32[3,4,16,128]{3,2,1,0:T(8,128)}) custom-call(s32[16]{0:T(128)} %shifts.1, f32[16]{0:T(128)} %viscosity.1, f32[4,16,128]{2,1,0:T(8,128)} %density.1, f32[4,16,128]{2,1,0:T(8,128)} %energy.1, f32[3,4,16,128]{3,2,1,0:T(8,128)} %velocity.1), custom_call_target="tpu_custom_call" | custom-call | tf_op jit(solution)/shard_map/disc_step/pallas_call | solution.py:292
  27.0 0.0 copy-start
  27.0 1.4 %copy.11 = f32[4,16,128]{2,1,0:T(8,128)} copy(f32[4,16,128]{2,1,0:T(8,128)} %get-tuple-element.6) | data formatting | bytes 65536
  28.4 1.4 %copy.12 = f32[4,16,128]{2,1,0:T(8,128)} copy(f32[4,16,128]{2,1,0:T(8,128)} %get-tuple-element.7) | data formatting | bytes 65536
  29.8 0.0 copy-done
  29.8 0.6 %copy.13 = f32[3,4,16,128]{3,2,1,0:T(8,128)} copy(f32[3,4,16,128]{3,2,1,0:T(8,128)S(1)} %copy-done) | data formatting | bytes 196608
Async XLA Ops:
  27.0 2.8 %copy-start = (f32[3,4,16,128]{3,2,1,0:T(8,128)S(1)}, f32[3,4,16,128]{3,2,1,0:T(8,128)}, u32[]{:S(2)}) copy-start(f32[3,4,16,128]{3,2,1,0:T(8,128)} %get-tuple-element.8) | copy-start | bytes 294916
